TPU v7x, 32 devices: a whole 2x2x4 slice. The times are simulated.
32 devices in a mesh: row: 4 (over y, x), col: 8 (over z, core).
Axes of the slice: x: 2, y: 2, z: 4, core: 2. Of those that a mesh axis runs over, the one named last changes fastest.
Arguments:
- psi: bfloat16 [8192, 8192], P(('row', 'col')), may hold values from -0.125 to 0.125
- hpsi: bfloat16 [8192, 128], P(('row', 'col')), may hold values from -0.796875 to 0.796875
- slab_counts: int32 [32], P(('row', 'col')), may hold values from 1 to 256, 6144 in all
- matrix: float32 [4, 2048, 8, 1024], P('row', None, 'col'), as said below
Outputs:
- reduced: float32 [4, 2048, 8, 1024], P('row', None, 'col')
Inputs may be any that keep to these rules, and one draw needn't show every extreme that they name: Slab k's live plane waves are its first slab_counts[k] slots; the rest are padding; the counts sum to 3 * 256 * 32 // 4. The stored matrix is symmetric.
All inputs are finite; a program needn't handle non-finite values.
Results may differ from a plain program's by a relative error of at most 0.0003.
Values sent between devices are 32-bit elements; how exact they have to be, the bound alone decides.
No kernel may reach another device: no remote copies, remote signals or barrier semaphores. Data moves between devices by JAX's collectives and lax.ppermute only.
A program may use at most 64 MiB of HBM per device.

v0:
```python
import jax
import jax.numpy as jnp
from jax import lax
from jax.sharding import PartitionSpec as P

TILE = 16
HIGH = lax.Precision.HIGHEST


def lower_solve(factor, rhs):
    return lax.linalg.triangular_solve(factor, rhs, left_side=True, lower=True)


def invert_shifted(shifted):
    normal = jnp.dot(shifted.T, shifted, precision=HIGH)
    factor = jnp.linalg.cholesky(normal)
    first = lower_solve(factor, shifted.T)
    return lax.linalg.triangular_solve(factor, first, left_side=True, lower=True, transpose_a=True)


def per_device(psi, hpsi, slab_counts, matrix):
    prow_id = lax.axis_index("row")
    pcol_id = lax.axis_index("col")
    n_row = lax.axis_size("row")
    n_col = lax.axis_size("col")
    slots = psi.shape[0]
    panel = hpsi.shape[1]
    local_rows = matrix.shape[1]
    local_cols = matrix.shape[3]
    tiles_r = local_rows // TILE
    tiles_c = local_cols // TILE
    valid = jnp.arange(slots, dtype=jnp.int32) < slab_counts[0]
    hcols = jnp.where(valid[:, None], hpsi, jnp.zeros_like(hpsi))
    local_r = jnp.arange(local_rows, dtype=jnp.int32)
    local_c = jnp.arange(local_cols, dtype=jnp.int32)
    row_global = (local_r // TILE * n_row + prow_id) * TILE + local_r % TILE
    col_global = (local_c // TILE * n_col + pcol_id) * TILE + local_c % TILE
    partial_value = lax.dot_general(
        psi, hcols, (((0,), (0,)), ((), ())), preferred_element_type=jnp.float32
    )
    whole = lax.psum(partial_value, ("row", "col"))
    prow = lax.dynamic_index_in_dim(
        whole.reshape(tiles_r, n_row, TILE, panel), prow_id, 1, keepdims=False
    ).reshape(local_rows, panel)
    scols = lax.dynamic_index_in_dim(
        whole.reshape(tiles_c, n_col, TILE, panel), pcol_id, 1, keepdims=False
    ).reshape(local_cols, panel)
    span = jnp.arange(panel, dtype=jnp.int32)
    lower_r = jnp.where((row_global >= panel)[:, None], prow, jnp.zeros_like(prow))
    lower_c = jnp.where((col_global >= panel)[:, None], scols, jnp.zeros_like(scols))
    top_select = (row_global[None, :] == panel + span[:, None]).astype(jnp.float32)
    gram_part = jnp.dot(lower_r.T, lower_r, precision=HIGH)
    top_part = jnp.dot(top_select, prow, precision=HIGH)
    gram, top_rows = lax.psum((gram_part, top_part), "row")
    factor = jnp.linalg.cholesky(gram)
    basis_r = lower_solve(factor, lower_r.T).T
    basis_c = lower_solve(factor, lower_c.T).T
    top = lower_solve(factor, top_rows.T).T
    inverse = invert_shifted(jnp.eye(panel, dtype=jnp.float32) - top)
    embed_r = (row_global[:, None] == panel + span[None, :]).astype(jnp.float32)
    embed_c = (col_global[:, None] == panel + span[None, :]).astype(jnp.float32)
    reflect_r = basis_r - embed_r
    reflect_c = basis_c - embed_c
    stored = matrix[0, :, 0, :]
    col_select = (col_global[None, :] == span[:, None]).astype(jnp.float32)
    row_select = (row_global[None, :] == span[:, None]).astype(jnp.float32)
    left = jnp.dot(prow, col_select, precision=HIGH)
    upper = lax.dot_general(row_select, scols, (((0,), (1,)), ((), ())), precision=HIGH)
    inside_r = (row_global < panel)[:, None]
    inside_c = (col_global < panel)[None, :]
    refreshed = jnp.where(
        inside_r & inside_c,
        0.5 * (left + upper),
        jnp.where(inside_c, left, jnp.where(inside_r, upper, stored)),
    )
    zpart = jnp.dot(refreshed, reflect_c, precision=HIGH)
    zrows = lax.psum(zpart, "col")
    upart = lax.dot_general(refreshed, reflect_r, (((0,), (0,)), ((), ())), precision=HIGH)
    ucols = lax.psum(upart, "row")
    wmat = lax.psum(jnp.dot(reflect_r.T, zrows, precision=HIGH), "row")
    core = jnp.dot(jnp.dot(inverse, wmat, precision=HIGH), inverse.T, precision=HIGH)
    first = jnp.dot(reflect_r, jnp.dot(inverse, ucols.T, precision=HIGH), precision=HIGH)
    second = jnp.dot(
        jnp.dot(zrows, inverse.T, precision=HIGH) - jnp.dot(reflect_r, core, precision=HIGH),
        reflect_c.T,
        precision=HIGH,
    )
    return (refreshed - first - second)[None, :, None, :]


def solution(mesh):
    in_specs = (
        P(("row", "col"), None),
        P(("row", "col"), None),
        P(("row", "col")),
        P("row", None, "col", None),
    )
    out_specs = P("row", None, "col", None)
    return jax.shard_map(
        per_device, mesh=mesh, in_specs=in_specs, out_specs=out_specs, check_vma=False
    )
```

profile of v0, /device:TPU:0, one launch (start us, length us, event | category | flops | bytes accessed | tf_op | source)
XLA Modules:
  0.0 421.6 jit_solution(14257435263756658271)
XLA Ops:
  7.2 5.1 %convolution_bitcast_fusion = f32[8192,128]{0,1:T(8,128)} fusion(bf16[256,8192]{1,0:T(8,128)(2,1)} %param.7, bf16[256,128]{1,0:T(8,128)(2,1)} %param.8, pred[256]{0:T(512)(128)(4,1)S(1)} %iota_compare_fusion.9), kind=kOutput, calls=%fused_computation | convolution fusion | flops 536903680 | bytes 8454400 | tf_op jit(solution)/shard_map/dot_general | solution.py:38
  12.3 0.0 all-reduce.6.cloned.1.call-update
  12.3 0.0 all-reduce.8.cloned.1.call-start
  12.5 0.1 fusion.18
  12.6 145.3 %all-reduce.6.cloned.1.call-done = f32[8192,128]{0,1:T(8,128)} async-done(((f32[8192,128]{0,1:T(8,128)}), f32[8192,128]{0,1:T(8,128)}) %all-reduce.6.cloned.1.call-update) | async-done | bytes 4194320 | tf_op jit(solution)/shard_map/psum | solution.py:41
  157.9 5.6 %copy.11 = f32[8192,128]{1,0:T(8,128)} copy(f32[8192,128]{0,1:T(8,128)} %all-reduce.6.cloned.1.call-done) | data formatting | bytes 8388608 | tf_op jit(solution)/shard_map/psum | solution.py:41
  163.4 1.6 broadcast_select_fusion
  165.0 2.4 convolution_bitcast_fusion.1
  167.5 0.0 all-reduce.8.cloned.1.call-update
  167.5 0.0 all-reduce.10.cloned.1.call-start
  167.5 3.6 fusion.10
  171.1 1.3 broadcast_select_fusion.1
  172.4 11.0 %fusion.1 = f32[2048,1024]{1,0:T(8,128)} fusion(f32[2048,1024]{1,0:T(8,128)S(1)} %fusion.10, f32[1,2048,1,1024]{3,2,1,0:T(1,128)} %param.10, pred[1024]{0:T(1024)(128)(4,1)S(1)} %broadcast_compare_fusion.1, pred[2048]{0:T(1024)(128)(4,1)S(1)} %broadcast_compare_fusion, f32[1024,128]{1,0:T(8,128)S(1)} %bitcast.89, s32[2048]{0:T(1024)S(1)} %fusion.60), kind=kOutput, calls=%fused_computation.3 | convolution fusion | flops 3234332672 | bytes 25701376 | tf_op jit(solution)/shard_map/dot_general | solution.py:68
  183.3 1.6 fusion.4
  185.0 23.8 %all-reduce.8.cloned.1.call-done = f32[128,128]{0,1:T(8,128)} async-done(((f32[128,128]{0,1:T(8,128)}), f32[128,128]{0,1:T(8,128)}) %all-reduce.8.cloned.1.call-update) | async-done | bytes 65552 | tf_op jit(solution)/shard_map/psum | solution.py:54
  208.8 0.9 copy.16
  209.7 0.9 fusion.29
  210.5 11.7 %cholesky.44 = f32[128,128]{1,0:T(8,128)S(1)} custom-call(f32[128,128]{1,0:T(8,128)S(1)} %fusion.29), custom_call_target="Cholesky" | custom-call | tf_op jit(solution)/shard_map/jit(cholesky)/cholesky | solution.py:55
  222.3 0.7 compare_reduce_fusion.1
  223.0 0.7 fusion.12
  223.7 9.8 %custom-call.13 = f32[1,128,128]{1,2,0:T(8,128)S(1)} custom-call(f32[1,128,128]{2,1,0:T(8,128)S(1)} %fusion.12), custom_call_target="InvertDiagBlocksLowerTriangular" | custom-call | tf_op jit(solution)/shard_map/triangular_solve | solution.py:11
  233.5 0.6 convolution_subtract_fusion.2
  234.1 10.1 %fusion.77 = f32[2048,128]{1,0:T(8,128)} fusion(f32[2048,1024]{1,0:T(8,128)} %fusion.1, f32[1024,128]{1,0:T(8,128)S(1)} %convolution_subtract_fusion.2), kind=kOutput, calls=%fused_computation.122 | convolution fusion | flops 3221225472 | bytes 9961472 | tf_op jit(solution)/shard_map/dot_general | solution.py:76
  244.2 0.0 all-reduce.10.cloned.1.call-update
  244.2 0.0 all-reduce.12.cloned.1.call-start
  244.2 1.0 convolution_subtract_fusion.1
  245.2 16.6 %fusion.74 = f32[1024,128]{1,0:T(8,128)} fusion(f32[2048,1024]{1,0:T(8,128)} %fusion.1, f32[2048,128]{1,0:T(8,128)S(1)} %convolution_subtract_fusion.1), kind=kOutput, calls=%fused_computation.119 | convolution fusion | flops 3221225472 | bytes 9961472 | tf_op jit(solution)/shard_map/dot_general | solution.py:78
  261.8 41.8 %all-reduce.10.cloned.1.call-done = f32[2048,128]{1,0:T(8,128)} async-done(((f32[2048,128]{1,0:T(8,128)}), f32[2048,128]{1,0:T(8,128)}) %all-reduce.10.cloned.1.call-update) | async-done | bytes 1048592 | tf_op jit(solution)/shard_map/psum | solution.py:77
  303.7 3.7 fusion.79
  307.3 0.0 all-reduce.12.cloned.1.call-update
  307.3 46.2 %all-reduce.12.cloned.1.call-done = (f32[128,128]{1,0:T(8,128)}, f32[1024,128]{1,0:T(8,128)}, f32[128,128]{1,0:T(8,128)}) async-done(((f32[128,128]{1,0:T(8,128)}, f32[1024,128]{1,0:T(8,128)}, f32[128,128]{1,0:T(8,128)}), (f32[128,128]{1,0:T(8,128)}, f32[1024,128]{1,0:T(8,128)}, f32[128,128]{1,0:T(8,128)})) %all-reduce.12.cloned.1.call-update) | async-done | bytes 655376 | tf_op jit(solution)/shard_map/psum | solution.py:54
  353.6 1.1 fusion.25
  354.7 0.3 fusion.24
  355.0 0.1 copy.17
  355.1 11.7 %cholesky.55 = f32[128,128]{1,0:T(8,128)S(1)} custom-call(f32[128,128]{1,0:T(8,128)S(1)} %fusion.23), custom_call_target="Cholesky" | custom-call | tf_op jit(solution)/shard_map/jit(cholesky)/cholesky | solution.py:16
  366.8 0.6 compare_reduce_fusion
  367.4 0.6 fusion.13
  368.0 9.8 %custom-call.14 = f32[1,128,128]{1,2,0:T(8,128)S(1)} custom-call(f32[1,128,128]{2,1,0:T(8,128)S(1)} %fusion.13), custom_call_target="InvertDiagBlocksLowerTriangular" | custom-call | tf_op jit(solution)/shard_map/triangular_solve | solution.py:18
  377.8 0.3 fusion.19
  378.1 0.2 fusion.21
  378.3 1.0 fusion.80
  379.4 0.3 fusion.81
  379.7 1.8 fusion.75
  381.4 7.2 %fusion.76 = f32[2048,1024]{1,0:T(8,128)S(1)} fusion(f32[2048,128]{1,0:T(8,128)S(1)} %convolution_subtract_fusion.1, f32[128,1024]{1,0:T(8,128)S(1)} %fusion.75), kind=kOutput, calls=%fused_computation.121 | convolution fusion | flops 3221225472 | bytes 9961472 | tf_op jit(solution)/shard_map/dot_general | solution.py:82
  388.7 1.0 fusion.78
  389.7 1.0 convolution_subtract_fusion
  390.7 8.0 %subtract_bitcast_fusion = f32[1,2048,1,1024]{3,1,2,0:T(8,128)S(1)} fusion(f32[2048,1024]{1,0:T(8,128)S(1)} %bitcast.83, f32[2048,1024]{1,0:T(8,128)S(1)} %fusion.76, f32[2048,128]{1,0:T(8,128)S(1)} %convolution_subtract_fusion, f32[1024,128]{1,0:T(8,128)S(1)} %convolution_subtract_fusion.2), kind=kOutput, calls=%fused_computation.4 | convolution fusion | flops 3225419776 | bytes 26738688 | tf_op jit(solution)/shard_map/dot_general | solution.py:83
  398.7 16.1 %copy.18 = f32[1,2048,1,1024]{3,2,1,0:T(1,128)} copy(f32[1,2048,1,1024]{3,1,2,0:T(8,128)S(1)} %subtract_bitcast_fusion) | data formatting | bytes 16777216 | tf_op jit(solution)/shard_map/broadcast_in_dim | solution.py:88
  (18 shorter events, 0.2 us)
Async XLA Ops:
  6.5 151.3 %all-reduce.6.cloned.1.call-start = ((), (), s32[]{:S(2)}) async-start(), calls=%async_computation | async-start | bytes 8388608 | tf_op jit(solution)/shard_map/psum | solution.py:41
  12.3 196.4 %all-reduce.8.cloned.1.call-start = ((), (), s32[]{:S(2)}) async-start(), calls=%async_computation.1 | async-start | bytes 131072 | tf_op jit(solution)/shard_map/psum | solution.py:54
  167.5 136.2 %all-reduce.10.cloned.1.call-start = ((), (), s32[]{:S(2)}) async-start(), calls=%async_computation.2 | async-start | bytes 2097152 | tf_op jit(solution)/shard_map/psum | solution.py:77
  244.2 109.4 %all-reduce.12.cloned.1.call-start = ((), (), s32[]{:S(2)}) async-start(), calls=%async_computation.3 | async-start | bytes 1310720 | tf_op jit(solution)/shard_map/psum | solution.py:54
  379.6 9.0 %copy-start = (f32[2048,128]{1,0:T(8,128)S(1)}, f32[2048,128]{1,0:T(8,128)}, u32[]{:S(2)}) copy-start(f32[2048,128]{1,0:T(8,128)} %all-reduce.10.cloned.1.call-done) | copy-start | bytes 3145732
  379.6 11.0 %slice-start = ((s8[8388608]{0:T(1024)(128)(4,1)}), s8[4194304]{0:T(1024)(128)(4,1)S(1)}, s32[]{:S(2)}) async-start(s8[8388608]{0:T(1024)(128)(4,1)} %bitcast.82), calls=%async_computation.4 | async-start | bytes 8388608
  381.4 9.3 %slice-start.1 = ((s8[8388608]{0:T(1024)(128)(4,1)}), s8[4194304]{0:T(1024)(128)(4,1)S(1)}, s32[]{:S(2)}) async-start(s8[8388608]{0:T(1024)(128)(4,1)} %bitcast.82), calls=%async_computation.5 | async-start | bytes 8388608
Sparse Core Ops, SparseCore 0:
  12.9 144.9 all-reduce.5
  167.6 41.1 all-reduce.7
  244.3 59.2 all-reduce.9
  307.5 46.0 all-reduce.11
where the time goes:
time: 428 us; the launch traced here: 422 us
  waiting for transfers between devices  257 us (60%)
  matrix products  77.7 us (18%)
  other arithmetic  49.6 us (12%)
  local copies, waits for them, and re-layouts  22.7 us (5%)
  between operations  14.3 us (3%)
    psum x1, waiting for transfers between devices, per_device(): whole = lax.psum(partial_value, ('row', 'col'))  145 us
    psum x2, waiting for transfers between devices, per_device(): gram, top_rows = lax.psum((gram_part, top_part), 'row')  70 us
    psum x1, waiting for transfers between devices, per_device(): zrows = lax.psum(zpart, 'col')  41.8 us
    dot_general x1, matrix products, per_device(): lax.dot_general(refreshed, reflect_r, (((0,), (0,)), ((), ())), precision...  16.6 us
    broadcast_in_dim x1, local copies, waits for them, and re-layouts, per_device(): return (refreshed - first - second)[None, :, None, :]  16.1 us
    another operation x3, other arithmetic, per_device(): factor = jnp.linalg.cholesky(gram)  12.5 us
    another operation x3, other arithmetic, invert_shifted(): factor = jnp.linalg.cholesky(normal)  12.4 us
    dot_general x1, matrix products, per_device(): lax.dot_general(row_select, scols, (((0,), (1,)), ((), ())), precision=HIGH)  11 us
  transfers between devices with their start and end apart: 4, of which 4 were waited for; matrix products, arithmetic and copies ran while one was open for 8% of the time, Pallas kernels for 0%

commit v1 on v0

--- a/solution.py
+++ b/solution.py
@@ -38,7 +38,9 @@
     partial_value = lax.dot_general(
         psi, hcols, (((0,), (0,)), ((), ())), preferred_element_type=jnp.float32
     )
-    whole = lax.psum(partial_value, ("row", "col"))
+    whole = partial_value
+    for axis in ("row", "col"):
+        whole = lax.psum(whole, axis)
     prow = lax.dynamic_index_in_dim(
         whole.reshape(tiles_r, n_row, TILE, panel), prow_id, 1, keepdims=False
     ).reshape(local_rows, panel)

time: 428 us -> 488 us (1.14)
  waiting for transfers between devices: 257 us -> 318 us
    psum x1 -> x2, waiting for transfers between devices: 145 us -> 205 us  [per_device(): whole = lax.psum(whole, axis)]
  transfers between devices with their start and end apart: 4 -> 5, of which waited for: 4 -> 5; matrix products, arithmetic and copies ran while one was open for 8% -> 7% of each run, Pallas kernels for 0% -> 0%
where the time goes in v1:
time: 488 us; the launch traced here: 482 us
  waiting for transfers between devices  318 us (65%)
  matrix products  77.7 us (16%)
  other arithmetic  49.6 us (10%)
  local copies, waits for them, and re-layouts  22.7 us (5%)
  between operations  14.3 us (3%)
    psum x2, waiting for transfers between devices, per_device(): whole = lax.psum(whole, axis)  205 us
    psum x2, waiting for transfers between devices, per_device(): gram, top_rows = lax.psum((gram_part, top_part), 'row')  70.8 us
    psum x1, waiting for transfers between devices, per_device(): zrows = lax.psum(zpart, 'col')  41.8 us
    dot_general x1, matrix products, per_device(): lax.dot_general(refreshed, reflect_r, (((0,), (0,)), ((), ())), precision...  16.6 us
    broadcast_in_dim x1, local copies, waits for them, and re-layouts, per_device(): return (refreshed - first - second)[None, :, None, :]  16.1 us
    another operation x3, other arithmetic, per_device(): factor = jnp.linalg.cholesky(gram)  12.5 us
    another operation x3, other arithmetic, invert_shifted(): factor = jnp.linalg.cholesky(normal)  12.4 us
    dot_general x1, matrix products, per_device(): lax.dot_general(row_select, scols, (((0,), (1,)), ((), ())), precision=HIGH)  11 us
  transfers between devices with their start and end apart: 5, of which 5 were waited for; matrix products, arithmetic and copies ran while one was open for 7% of the time, Pallas kernels for 0%

profile of v1, /device:TPU:0, one launch (start us, length us, event | category | flops | bytes accessed | tf_op | source)
XLA Modules:
  0.0 482.1 jit_solution(243958844398236610)
XLA Ops:
  7.2 5.1 %convolution_bitcast_fusion = f32[8192,128]{0,1:T(8,128)} fusion(bf16[256,8192]{1,0:T(8,128)(2,1)} %param.7, bf16[256,128]{1,0:T(8,128)(2,1)} %param.8, pred[256]{0:T(512)(128)(4,1)S(1)} %iota_compare_fusion.9), kind=kOutput, calls=%fused_computation | convolution fusion | flops 536903680 | bytes 8454400 | tf_op jit(solution)/shard_map/dot_general | solution.py:38
  12.3 0.0 all-reduce.7.cloned.1.call-update
  12.3 0.0 all-reduce.9.cloned.1.call-start
  12.4 106.4 %all-reduce.7.cloned.1.call-done = f32[8192,128]{0,1:T(8,128)} async-done(((f32[8192,128]{0,1:T(8,128)}), f32[8192,128]{0,1:T(8,128)}) %all-reduce.7.cloned.1.call-update) | async-done | bytes 4194320 | tf_op jit(solution)/shard_map/psum | solution.py:43
  118.8 0.0 all-reduce.9.cloned.1.call-update
  118.8 0.0 all-reduce.11.cloned.1.call-start
  119.0 0.1 fusion.18
  119.1 98.6 %all-reduce.9.cloned.1.call-done = f32[8192,128]{0,1:T(8,128)} async-done(((f32[8192,128]{0,1:T(8,128)}), f32[8192,128]{0,1:T(8,128)}) %all-reduce.9.cloned.1.call-update) | async-done | bytes 4194320 | tf_op jit(solution)/shard_map/psum | solution.py:43
  217.7 5.6 %copy.11 = f32[8192,128]{1,0:T(8,128)} copy(f32[8192,128]{0,1:T(8,128)} %all-reduce.9.cloned.1.call-done) | data formatting | bytes 8388608 | tf_op jit(solution)/shard_map/psum | solution.py:43
  223.2 1.6 broadcast_select_fusion
  224.8 2.4 convolution_bitcast_fusion.1
  227.3 0.0 all-reduce.13.cloned.1.call-start
  227.3 3.6 fusion.10
  230.9 1.3 broadcast_select_fusion.1
  232.2 11.0 %fusion.1 = f32[2048,1024]{1,0:T(8,128)} fusion(f32[2048,1024]{1,0:T(8,128)S(1)} %fusion.10, f32[1,2048,1,1024]{3,2,1,0:T(1,128)} %param.10, pred[1024]{0:T(1024)(128)(4,1)S(1)} %broadcast_compare_fusion.1, pred[2048]{0:T(1024)(128)(4,1)S(1)} %broadcast_compare_fusion, f32[1024,128]{1,0:T(8,128)S(1)} %bitcast.89, s32[2048]{0:T(1024)S(1)} %fusion.60), kind=kOutput, calls=%fused_computation.3 | convolution fusion | flops 3234332672 | bytes 25701376 | tf_op jit(solution)/shard_map/dot_general | solution.py:70
  243.2 1.6 fusion.4
  244.8 24.5 %all-reduce.11.cloned.1.call-done = f32[128,128]{0,1:T(8,128)} async-done(((f32[128,128]{0,1:T(8,128)}), f32[128,128]{0,1:T(8,128)}) %all-reduce.11.cloned.1.call-update) | async-done | bytes 65552 | tf_op jit(solution)/shard_map/psum | solution.py:56
  269.3 0.9 copy.16
  270.3 0.9 fusion.29
  271.1 11.7 %cholesky.44 = f32[128,128]{1,0:T(8,128)S(1)} custom-call(f32[128,128]{1,0:T(8,128)S(1)} %fusion.29), custom_call_target="Cholesky" | custom-call | tf_op jit(solution)/shard_map/jit(cholesky)/cholesky | solution.py:57
  282.9 0.7 compare_reduce_fusion.1
  283.6 0.7 fusion.12
  284.3 9.8 %custom-call.13 = f32[1,128,128]{1,2,0:T(8,128)S(1)} custom-call(f32[1,128,128]{2,1,0:T(8,128)S(1)} %fusion.12), custom_call_target="InvertDiagBlocksLowerTriangular" | custom-call | tf_op jit(solution)/shard_map/triangular_solve | solution.py:11
  294.1 0.6 convolution_subtract_fusion.2
  294.7 10.1 %fusion.77 = f32[2048,128]{1,0:T(8,128)} fusion(f32[2048,1024]{1,0:T(8,128)} %fusion.1, f32[1024,128]{1,0:T(8,128)S(1)} %convolution_subtract_fusion.2), kind=kOutput, calls=%fused_computation.122 | convolution fusion | flops 3221225472 | bytes 9961472 | tf_op jit(solution)/shard_map/dot_general | solution.py:78
  304.8 0.0 all-reduce.15.cloned.1.call-start
  304.8 1.0 convolution_subtract_fusion.1
  305.8 16.6 %fusion.74 = f32[1024,128]{1,0:T(8,128)} fusion(f32[2048,1024]{1,0:T(8,128)} %fusion.1, f32[2048,128]{1,0:T(8,128)S(1)} %convolution_subtract_fusion.1), kind=kOutput, calls=%fused_computation.119 | convolution fusion | flops 3221225472 | bytes 9961472 | tf_op jit(solution)/shard_map/dot_general | solution.py:80
  322.4 41.8 %all-reduce.13.cloned.1.call-done = f32[2048,128]{1,0:T(8,128)} async-done(((f32[2048,128]{1,0:T(8,128)}), f32[2048,128]{1,0:T(8,128)}) %all-reduce.13.cloned.1.call-update) | async-done | bytes 1048592 | tf_op jit(solution)/shard_map/psum | solution.py:79
  364.2 3.7 fusion.79
  367.9 46.2 %all-reduce.15.cloned.1.call-done = (f32[128,128]{1,0:T(8,128)}, f32[1024,128]{1,0:T(8,128)}, f32[128,128]{1,0:T(8,128)}) async-done(((f32[128,128]{1,0:T(8,128)}, f32[1024,128]{1,0:T(8,128)}, f32[128,128]{1,0:T(8,128)}), (f32[128,128]{1,0:T(8,128)}, f32[1024,128]{1,0:T(8,128)}, f32[128,128]{1,0:T(8,128)})) %all-reduce.15.cloned.1.call-update) | async-done | bytes 655376 | tf_op jit(solution)/shard_map/psum | solution.py:56
  414.1 1.1 fusion.25
  415.3 0.3 fusion.24
  415.5 0.1 copy.17
  415.7 11.7 %cholesky.55 = f32[128,128]{1,0:T(8,128)S(1)} custom-call(f32[128,128]{1,0:T(8,128)S(1)} %fusion.23), custom_call_target="Cholesky" | custom-call | tf_op jit(solution)/shard_map/jit(cholesky)/cholesky | solution.py:16
  427.4 0.6 compare_reduce_fusion
  428.0 0.6 fusion.13
  428.6 9.8 %custom-call.14 = f32[1,128,128]{1,2,0:T(8,128)S(1)} custom-call(f32[1,128,128]{2,1,0:T(8,128)S(1)} %fusion.13), custom_call_target="InvertDiagBlocksLowerTriangular" | custom-call | tf_op jit(solution)/shard_map/triangular_solve | solution.py:18
  438.4 0.3 fusion.19
  438.7 0.2 fusion.21
  438.9 1.0 fusion.80
  440.0 0.3 fusion.81
  440.2 1.8 fusion.75
  442.0 7.2 %fusion.76 = f32[2048,1024]{1,0:T(8,128)S(1)} fusion(f32[2048,128]{1,0:T(8,128)S(1)} %convolution_subtract_fusion.1, f32[128,1024]{1,0:T(8,128)S(1)} %fusion.75), kind=kOutput, calls=%fused_computation.121 | convolution fusion | flops 3221225472 | bytes 9961472 | tf_op jit(solution)/shard_map/dot_general | solution.py:84
  449.3 1.0 fusion.78
  450.3 1.0 convolution_subtract_fusion
  451.3 8.0 %subtract_bitcast_fusion = f32[1,2048,1,1024]{3,1,2,0:T(8,128)S(1)} fusion(f32[2048,1024]{1,0:T(8,128)S(1)} %bitcast.83, f32[2048,1024]{1,0:T(8,128)S(1)} %fusion.76, f32[2048,128]{1,0:T(8,128)S(1)} %convolution_subtract_fusion, f32[1024,128]{1,0:T(8,128)S(1)} %convolution_subtract_fusion.2), kind=kOutput, calls=%fused_computation.4 | convolution fusion | flops 3225419776 | bytes 26738688 | tf_op jit(solution)/shard_map/dot_general | solution.py:85
  459.3 16.1 %copy.18 = f32[1,2048,1,1024]{3,2,1,0:T(1,128)} copy(f32[1,2048,1,1024]{3,1,2,0:T(8,128)S(1)} %subtract_bitcast_fusion) | data formatting | bytes 16777216 | tf_op jit(solution)/shard_map/broadcast_in_dim | solution.py:90
  (21 shorter events, 0.2 us)
Async XLA Ops:
  6.5 112.3 %all-reduce.7.cloned.1.call-start = ((), (), s32[]{:S(2)}) async-start(), calls=%async_computation | async-start | bytes 8388608 | tf_op jit(solution)/shard_map/psum | solution.py:43
  12.3 205.4 %all-reduce.9.cloned.1.call-start = ((), (), s32[]{:S(2)}) async-start(), calls=%async_computation.1 | async-start | bytes 8388608 | tf_op jit(solution)/shard_map/psum | solution.py:43
  118.8 150.5 %all-reduce.11.cloned.1.call-start = ((), (), s32[]{:S(2)}) async-start(), calls=%async_computation.2 | async-start | bytes 131072 | tf_op jit(solution)/shard_map/psum | solution.py:56
  227.3 136.9 %all-reduce.13.cloned.1.call-start = ((), (), s32[]{:S(2)}) async-start(), calls=%async_computation.3 | async-start | bytes 2097152 | tf_op jit(solution)/shard_map/psum | solution.py:79
  304.8 109.4 %all-reduce.15.cloned.1.call-start = ((), (), s32[]{:S(2)}) async-start(), calls=%async_computation.4 | async-start | bytes 1310720 | tf_op jit(solution)/shard_map/psum | solution.py:56
  440.2 9.0 %copy-start = (f32[2048,128]{1,0:T(8,128)S(1)}, f32[2048,128]{1,0:T(8,128)}, u32[]{:S(2)}) copy-start(f32[2048,128]{1,0:T(8,128)} %all-reduce.13.cloned.1.call-done) | copy-start | bytes 3145732
  440.2 11.0 %slice-start = ((s8[8388608]{0:T(1024)(128)(4,1)}), s8[4194304]{0:T(1024)(128)(4,1)S(1)}, s32[]{:S(2)}) async-start(s8[8388608]{0:T(1024)(128)(4,1)} %bitcast.82), calls=%async_computation.5 | async-start | bytes 8388608
  442.0 9.3 %slice-start.1 = ((s8[8388608]{0:T(1024)(128)(4,1)}), s8[4194304]{0:T(1024)(128)(4,1)S(1)}, s32[]{:S(2)}) async-start(s8[8388608]{0:T(1024)(128)(4,1)} %bitcast.82), calls=%async_computation.6 | async-start | bytes 8388608
Sparse Core Ops, SparseCore 0:
  12.4 106.3 all-reduce.6
  121.2 96.4 all-reduce.8
  227.4 41.8 all-reduce.10
  304.9 59.2 all-reduce.12
  368.0 46.0 all-reduce.14
